TPU v7x, 32 devices: a whole 2x2x4 slice. The times are simulated.
32 devices in a mesh: rep: 4 (over z), fsdp: 8 (over y, x, core).
Axes of the slice: x: 2, y: 2, z: 4, core: 2. Of those that a mesh axis runs over, the one named last changes fastest.
Arguments:
- x_tokens: bfloat16 [256, 257, 1024], P(('rep', 'fsdp'))
- grad_z: bfloat16 [256, 257, 1024], P(('rep', 'fsdp'))
- w_qkv: float32 [1024, 3072], P('fsdp')
- b_qkv: float32 [3072], P('fsdp')
- w_out: float32 [1024, 1024], P('fsdp')
- w_up: float32 [1024, 4096], P('fsdp')
- b_up: float32 [4096], P('fsdp')
- w_down: float32 [4096, 1024], P('fsdp')
- vec_params: float32 [8, 1024], P(None, 'fsdp')
Outputs:
- output 1: bfloat16 [256, 257, 1024], P(('rep', 'fsdp'))
- output 2: bfloat16 [256, 257, 1024], P(('rep', 'fsdp'))
- output 3: float32 [1024, 3072], P('fsdp')
- output 4: float32 [3072], P('fsdp')
- output 5: float32 [1024, 1024], P('fsdp')
- output 6: float32 [1024, 4096], P('fsdp')
- output 7: float32 [4096], P('fsdp')
- output 8: float32 [4096, 1024], P('fsdp')
- output 9: float32 [8, 1024], P(None, 'fsdp')
All inputs are finite; a program needn't handle non-finite values.
Results may differ from a plain program's by a relative error of at most 0.02.
Values are sent between devices in bfloat16 or wider.
A program may use at most 1 GiB of HBM per device.

v0:
```python
import functools
import itertools

import jax
import jax.numpy as jnp
from jax import lax
from jax.experimental import pallas as pl
from jax.experimental.pallas import tpu as pltpu
from jax.sharding import PartitionSpec as P

F32 = jnp.float32
BF16 = jnp.bfloat16
LN_EPS = 1e-5
HEADS = 16
D = 1024
SEQ = 257
NSEQ = 8
PAD = 272
MAIN = 256
TAIL = PAD - MAIN
HEAD = D // HEADS
SCALE = HEAD ** -0.5
LOG2E = 1.4426950408889634
NEG = -1e30
QTR = 1024
ROWS = 128
LANES = 128
HD = D // 2
HH = HEADS // 2
PEERS = 8
DEPTH = 4
VMEM_MAX = 62 * 1024 * 1024
MESH = pl.DeviceIdType.MESH
ANY = pl.BlockSpec(memory_space=pl.ANY)
V_UP, V_QKV = 8, 12


def dot_nn(a, b):
    return lax.dot_general(a, b, (((1,), (0,)), ((), ())), preferred_element_type=F32)


def dot_nt(a, b):
    return lax.dot_general(a, b, (((1,), (1,)), ((), ())), preferred_element_type=F32)


def dot_tn(a, b):
    return lax.dot_general(a, b, (((0,), (0,)), ((), ())), preferred_element_type=F32)


def row_mean(t):
    return jnp.mean(t, axis=-1, keepdims=True)


def col_sum(t):
    return jnp.sum(t, axis=0, keepdims=True)


def ln_fwd(t):
    cen = t - row_mean(t)
    rstd = lax.rsqrt(row_mean(cen * cen) + LN_EPS)
    return cen * rstd, rstd


def ln_bwd(dxhat, xhat, rstd):
    return rstd * (dxhat - row_mean(dxhat) - xhat * row_mean(dxhat * xhat))


def sub8(t):
    return jnp.sum(t.reshape(t.shape[0] // 8, 8, t.shape[1]), axis=0)


def table_rows(ref, first=0, count=8):
    return [ref[k:k + 1] for k in range(first, first + count)]


def block(k):
    return slice(k * LANES, (k + 1) * LANES)


def params():
    return pltpu.CompilerParams(dimension_semantics=("arbitrary",), vmem_limit_bytes=VMEM_MAX)


def comm_params(cid):
    return pltpu.CompilerParams(dimension_semantics=("arbitrary",), vmem_limit_bytes=VMEM_MAX,
                                collective_id=cid, has_side_effects=True)


def fixed(shape):
    zeros = (0,) * len(shape)
    return pl.BlockSpec(shape, lambda *_: zeros, pipeline_mode=pl.Buffered(1))


def resident(shape):
    zeros = (0,) * len(shape)
    return pl.BlockSpec(shape, lambda *_: zeros)


def wblk(i):
    return pl.BlockSpec((PEERS, ROWS, D), lambda *_: (0, i, 0), pipeline_mode=pl.Buffered(1))


def one_seq(width=D, col=0):
    return pl.BlockSpec((None, PAD, width), lambda s: (s, 0, col))


def act(width=D, dtype=BF16):
    return jax.ShapeDtypeStruct((NSEQ, PAD, width), dtype)


def f32s(*shape):
    return jax.ShapeDtypeStruct(shape, F32)


def coords():
    me, z = lax.axis_index("fsdp"), lax.axis_index("rep")
    return z, me // 4, lax.rem(me // 2, 2), lax.rem(me, 2)


def index_of(name):
    _, y, x, c = coords()
    if "core" in name:
        c = 1 - c
    if "x" in name:
        x = 1 - x
    if "y" in name:
        y = 1 - y
    return 4 * y + 2 * x + c


def partner(name):
    z = lax.axis_index("rep")
    if name == "near":
        z = z + 1 - 2 * lax.rem(z, 2)
    elif name == "far":
        z = 3 - z
    return (z, index_of(name if name in ("core", "x", "y") else ""))


def is_inner():
    z = lax.axis_index("rep")
    return lax.rem(z + z // 2, 2)


def greet(devices, extra=0):
    sem = pltpu.get_barrier_semaphore()
    for dev in devices:
        pl.semaphore_signal(sem, inc=1, device_id=dev, device_id_type=MESH)
    pl.semaphore_wait(sem, len(devices) + extra)


def barrier(names):
    far = "far" in names
    inner = is_inner()
    if far:
        @pl.when(inner == 1)
        def _():
            pl.semaphore_signal(pltpu.get_barrier_semaphore(), inc=1, device_id=partner("far"), device_id_type=MESH)
    greet([partner(name) for name in names if name != "far"], inner if far else 0)


def remote(src, dst, sems, k, device):
    send_sem, recv_sem = sems
    return pltpu.make_async_remote_copy(src_ref=src, dst_ref=dst, send_sem=send_sem.at[k], recv_sem=recv_sem.at[k],
                                        device_id=device, device_id_type=MESH)


class Move:
    def __init__(self, copy, sender="every", receiver="every"):
        self.copy, self.sender, self.receiver = copy, sender, receiver

    def role(self, who, do):
        if who == "every":
            do()
        else:
            pl.when(is_inner() == int(who == "inner"))(do)

    def start(self):
        self.role(self.sender, self.copy.start)

    def recv(self):
        self.role(self.receiver, self.copy.wait_recv)

    def sent(self):
        self.role(self.sender, self.copy.wait_send)


ROLES = {"zA": ("outer", "inner"), "zB": ("inner", "inner"), "zC": ("inner", "outer")}
NAMES = {"s1": ("x", "y"), "s2": ("y", "x"), "zA": ("near", "near"), "zB": ("far", "far"), "zC": ("near", "near"),
         "gather": ("core", "x", "y")}
GATHER_COPIES = 8
END = -1
ONCE = 1


def passes(shape):
    return shape[:1] + shape[2:] if len(shape) > 4 else shape


def kept_spec(shape):
    full = (shape[0], 1) + shape[2:] if len(shape) > 4 else shape
    zeros = (0,) * len(shape)
    return pl.BlockSpec(full, lambda *_: zeros, pipeline_mode=pl.Buffered(1))


class Chain:
    def __init__(self, array, first, *plan):
        self.array = array
        self.stages = [first] + [st for st, *_ in plan]
        self.steps = [(0, 0)] + [(steps[0], steps[-1]) for _, *steps in plan]
        self.ends = self.stages[-1] == "zC"
        self.many = len(self.stages) > 1
        self.names = [nm for st in self.stages for nm in NAMES[st]]
        self.held = []
        shape = array.shape
        for _ in plan:
            shape = passes(shape)
            self.held.append(shape)
        self.kept, self.last = passes(shape), passes(shape)

    def args(self):
        return [self.array] * (1 + self.many)

    def in_specs(self):
        return [ANY, kept_spec(self.array.shape)][:1 + self.many]

    def results(self):
        kept = [(fixed(self.kept), self.kept)] * self.many
        return kept if self.many and self.ends else kept + [(ANY, self.last)]

    def scratch(self):
        return [pltpu.VMEM(shape, F32) for shape in self.held]

    def bind(self, ins, outs, held, sems, k):
        self.kept_out = outs[0]
        sources = ins[:1] + held
        targets = held + ([held[-1]] if self.many and self.ends else outs[-1:])
        if self.ends and not self.many:
            sources = outs[-1:]
        self.sums, self.adds, self.moves = held, ins[1:] + held, []
        for st, src, dst in zip(self.stages, sources, targets):
            moves = []
            for color, name in enumerate(NAMES[st]):
                a = src.at[color, 1] if st in ("s1", "s2") else src.at[color]
                moves.append(Move(remote(a, dst.at[color], sems, k, partner(name)), *ROLES.get(st, ())))
                k += 1
            self.moves.append(moves)
        return k

    def pass_on(self, n, color):
        if n:
            self.moves[n - 1][color].recv()
            held, kept = self.sums[n - 1], self.adds[n - 1]

            def add():
                mine = kept[color, 0] if len(kept.shape) > len(held.shape) else kept[color]
                held[color] = held[color] + mine
            if self.stages[n - 1] in ROLES:
                pl.when(is_inner() == 1)(add)
            else:
                add()
        self.moves[n][color].start()

    def step(self, i):
        for n, steps in enumerate(self.steps):
            for color, step in enumerate(steps):
                @pl.when(i == step)
                def _(n=n, color=color):
                    self.pass_on(n, color)

    def finish(self):
        for mv in self.moves[-1]:
            mv.recv()
        if self.many:
            held = self.sums[-1]
            self.kept_out[:] = held[:, 0] if len(held.shape) > len(self.kept) else held[:]
        for moves in self.moves:
            for mv in moves:
                mv.sent()


class Gather:
    names = NAMES["gather"]

    def __init__(self, buf, first, *steps, start=0):
        self.buf, self.plan = buf, [(first + j, step) for j, step in enumerate((start,) + steps)]

    def args(self):
        return [self.buf]

    def in_specs(self):
        return [ANY]

    def results(self):
        return [(ANY, self.buf.shape)]

    def scratch(self):
        return []

    def bind(self, ins, outs, held, sems, k):
        self.rounds = gather_moves(outs[0], sems, k)
        return k + GATHER_COPIES

    def step(self, i):
        for j, (rnd, step) in enumerate(self.plan):
            @pl.when(i == step)
            def _(j=j, rnd=rnd):
                if j:
                    pass_on([self.rounds], rnd)
                else:
                    for mv in self.rounds[rnd].every:
                        mv.start()

    def finish(self):
        for rnd, step in self.plan:
            if step == END:
                pass_on([self.rounds], rnd)
        for j, (rnd, _) in enumerate(self.plan):
            for mv in self.rounds[rnd].kept if j + 1 < len(self.plan) else self.rounds[rnd].every:
                mv.recv()
            for mv in self.rounds[rnd].every:
                mv.sent()


class Traffic:
    def __init__(self, items=(), extra=()):
        self.items = list(items)
        self.names = sorted({nm for item in self.items for nm in item.names} | set(extra))
        self.count = sum(GATHER_COPIES if isinstance(item, Gather) else len(item.names) for item in self.items)

    def arrays(self):
        return [arr for item in self.items for arr in item.args()]

    def in_specs(self):
        return [spec for item in self.items for spec in item.in_specs()]

    def out_specs(self):
        return [spec for item in self.items for spec, _ in item.results()]

    def out_shapes(self):
        return [jax.ShapeDtypeStruct(shape, item.args()[0].dtype) for item in self.items for _, shape in item.results()]

    def scratch(self):
        n = max(self.count, 1)
        held = [each for item in self.items for each in item.scratch()]
        return held + [pltpu.SemaphoreType.DMA((n,)), pltpu.SemaphoreType.DMA((n,))]

    def sizes(self):
        return len(self.in_specs()), len(self.out_specs()), len(self.scratch())

    def aliases(self, ins, outs):
        pairs = {}
        for item in self.items:
            if isinstance(item, Gather) or (item.ends and not item.many):
                pairs[ins] = outs
            ins, outs = ins + len(item.in_specs()), outs + len(item.results())
        return pairs

    def split(self, results):
        results, out = list(results), []
        for item in self.items:
            n = len(item.results())
            out.append(results[0] if n == 1 else tuple(results[:n]))
            results = results[n:]
        return out

    def begin(self, i, ins, outs, scratch):
        ins, outs, scratch = list(ins), list(outs), list(scratch)
        *scratch, send_sem, recv_sem = scratch
        k = 0
        for item in self.items:
            n, m, h = len(item.in_specs()), len(item.results()), len(item.scratch())
            k = item.bind(ins[:n], outs[:m], scratch[:h], (send_sem, recv_sem), k)
            ins, outs, scratch = ins[n:], outs[m:], scratch[h:]
        if self.names:
            @pl.when(i == 0)
            def _():
                barrier(self.names)
        for item in self.items:
            item.step(i)

    def finish(self, last):
        if self.items:
            @pl.when(last)
            def _():
                for item in self.items:
                    item.finish()


def pass_on(gathers, rnd):
    for rounds in gathers:
        for mv in rounds[rnd - 1].passed_on:
            mv.recv()
        for mv in rounds[rnd].every:
            mv.start()


class Round:
    def __init__(self, kept, passed_on):
        self.kept, self.passed_on, self.every = kept, passed_on, kept + passed_on


def gather_moves(buf, sems, k, own=None, rows=slice(None), half=None):
    n = buf.shape[1]
    me, at_x, at_y, at_xy = index_of(""), index_of("x"), index_of("y"), index_of("xy")
    low, high = half or (slice(0, n // 2), slice(n // 2, n))

    def mv(j, src, dst, name):
        return Move(remote(src, dst, sems, k + j, partner(name)))

    mine = buf.at[me, rows]
    first = [mv(j, mine if own is None else own, mine, name) for j, name in enumerate(NAMES["gather"])]
    second = [(at_x, rows, "core"), (at_y, rows, "core"), (at_y, low, "x"), (at_x, high, "y")]
    second = [mv(len(first) + j, buf.at[who, part], buf.at[who, part], name) for j, (who, part, name) in enumerate(second)]
    last = buf.at[at_xy, rows]
    third = [mv(len(first) + len(second), last, last, "core")]
    return Round(first[:1], first[1:]), Round(second[:2], second[2:]), Round(third, [])


def intake_kernel(xt, gt, wq, wo, wup, wdown, vecs, xp_ref, gp_ref, wall, wo_buf, *refs):
    (*ff_bufs, table_ref, xs, wide, wq_s, wo_s, up_s, down_s, own, ff_own, all_v,
     ssem, rsem, lsem) = refs
    me = index_of("")
    z = lax.axis_index("rep")
    loads = [pltpu.make_async_copy(src, dst, lsem.at[k]) for k, (src, dst) in enumerate((
        (wq, wq_s), (wo, wo_s), (wup, up_s), (wdown, down_s), (xt, xs.at[0]), (gt, xs.at[1])))]
    get_wq, get_wo, get_up, get_down, get_x, get_g = loads
    for cp in loads:
        cp.start()
    greet([(z, lax.rem(me + k, PEERS)) for k in range(1, PEERS)])
    vec_moves = [Move(remote(vecs, all_v.at[me], (ssem, rsem), k - 1, (z, lax.rem(me + k, PEERS))))
                 for k in range(1, PEERS)]
    for mv in vec_moves:
        mv.start()
    all_v[me] = vecs[:]
    get_wq.wait()
    stores, rounds = [], []

    def store(src, dst):
        cp = pltpu.make_async_copy(src, dst, lsem.at[len(loads) + len(stores)])
        cp.start()
        stores.append(cp)

    for t in range(3):
        part = slice(t * ROWS, (t + 1) * ROWS)
        own[part] = wq_s[:, t * D:(t + 1) * D].astype(BF16)
        mid = t * ROWS + ROWS // 2
        rounds.append(gather_moves(wall, (ssem, rsem), PEERS - 1 + t * GATHER_COPIES, own.at[part], part,
                                   (slice(t * ROWS, mid), slice(mid, (t + 1) * ROWS))))
        for mv in rounds[t][0].every:
            mv.start()
    store(own, wall.at[me])

    get_wo.wait()
    ff_own[DEPTH, :ROWS] = wo_s[:].astype(BF16)
    store(ff_own.at[DEPTH, pl.ds(0, ROWS)], wo_buf.at[me])
    get_up.wait()
    get_down.wait()
    for j, buf in enumerate(ff_bufs):
        for k in range(PEERS):
            ff_own[j, :ROWS, block(k)] = up_s[:, block(DEPTH * k + j)].astype(BF16)
        ff_own[j, ROWS:] = down_s[j * ROWS:(j + 1) * ROWS].astype(BF16)
        store(ff_own.at[j], buf.at[me])

    def by_sequence(t, out_ref):
        for k in range(PEERS):
            wide[k] = xs[t, :, :, block(k)].astype(F32).reshape(SEQ * NSEQ, LANES)
        out_ref[:, MAIN:PAD] = jnp.zeros((NSEQ, TAIL, D), BF16)

        @pl.loop(0, NSEQ)
        def _(s):
            for k in range(PEERS):
                out_ref[s, pl.ds(0, SEQ), block(k)] = wide[k, pl.ds(s, SEQ, stride=NSEQ), :].astype(BF16)

    get_x.wait()
    by_sequence(0, xp_ref)
    pass_on(rounds[:1], 1)
    get_g.wait()
    by_sequence(1, gp_ref)
    pass_on(rounds[1:], 1)
    for mv in vec_moves:
        mv.recv()
    for r in range(V_QKV):
        table_ref[r:r + 1] = jnp.concatenate([all_v[k, r:r + 1] for k in range(PEERS)], axis=1)
    flat = [all_v[k, V_QKV + t:V_QKV + t + 1] for k in range(PEERS) for t in range(3)]
    for t in range(3):
        table_ref[V_QKV + t:V_QKV + t + 1] = jnp.concatenate(flat[t * PEERS:(t + 1) * PEERS], axis=1)
    table_ref[:] = table_ref[:].astype(BF16).astype(F32)
    pass_on(rounds, 2)
    for first, second, third in rounds:
        for mv in first.kept + second.kept + third.every:
            mv.recv()
        for mv in first.every + second.every + third.every:
            mv.sent()
    for mv in vec_moves:
        mv.sent()
    for cp in stores:
        cp.wait()


def run_intake(xt, gt, wq, wo, wup, wdown, vecs, cid):
    copies = PEERS - 1 + 3 * GATHER_COPIES
    bufs = [jax.ShapeDtypeStruct((PEERS, n * ROWS, D), BF16) for n in (3, 1) + (2,) * DEPTH]
    vmem = pltpu.VMEM
    return pl.pallas_call(
        intake_kernel,
        in_specs=[ANY] * 6 + [pl.BlockSpec(memory_space=vmem)],
        out_specs=[pl.BlockSpec(memory_space=vmem)] * 2 + [ANY] * len(bufs) + [pl.BlockSpec(memory_space=vmem)],
        out_shape=[act(), act()] + bufs + [f32s(16, D)],
        scratch_shapes=[vmem((2, SEQ, NSEQ, D), BF16), vmem((PEERS, SEQ * NSEQ, LANES), F32),
                        vmem(wq.shape, F32), vmem(wo.shape, F32), vmem(wup.shape, F32), vmem(wdown.shape, F32),
                        vmem((3 * ROWS, D), BF16), vmem((DEPTH + 1, 2 * ROWS, D), BF16), vmem((PEERS, 16, LANES), F32),
                        pltpu.SemaphoreType.DMA((copies,)), pltpu.SemaphoreType.DMA((copies,)),
                        pltpu.SemaphoreType.DMA((6 + 2 + DEPTH,))],
        compiler_params=pltpu.CompilerParams(vmem_limit_bytes=VMEM_MAX, collective_id=cid, has_side_effects=True),
        name="intake",
    )(xt, gt, wq, wo, wup, wdown, vecs)


def qkv_kernel(traffic, x_ref, wq_ref, wk_ref, wv_ref, vec_ref, *refs):
    n_in, n_out, _ = traffic.sizes()
    srcs, (h_ref, q_ref, k_ref, v_ref, *refs) = refs[:n_in], refs[n_in:]
    i = pl.program_id(0)
    traffic.begin(i, srcs, refs[:n_out], refs[n_out:])
    rows = x_ref.shape[0] * PAD
    g1, c1, *_ = table_rows(vec_ref)
    xhat, _ = ln_fwd(x_ref[:].reshape(rows, D).astype(F32))
    h = (xhat * g1 + c1).astype(BF16)
    h_ref[:] = h.reshape(h_ref.shape)
    biases = table_rows(vec_ref, V_QKV, 3)
    for w_ref, o_ref, bias in zip((wq_ref, wk_ref, wv_ref), (q_ref, k_ref, v_ref), biases):
        o_ref[:] = (dot_nn(h, w_ref[:].reshape(D, D)) + bias).astype(BF16).reshape(o_ref.shape)
    traffic.finish(i == pl.num_programs(0) - 1)


def run_qkv(xp, wall, vec, cid, items):
    bs = 2
    traffic = Traffic(items)
    tok = pl.BlockSpec((bs, PAD, D), lambda s: (s, 0, 0))
    outs = pl.pallas_call(
        functools.partial(qkv_kernel, traffic), grid=(NSEQ // bs,),
        in_specs=[tok, *map(wblk, range(3)), fixed(vec.shape)] + traffic.in_specs(),
        out_specs=[tok] * 4 + traffic.out_specs(), out_shape=[act()] * 4 + traffic.out_shapes(),
        scratch_shapes=traffic.scratch(), input_output_aliases=traffic.aliases(5, 4),
        compiler_params=comm_params(cid), name="qkv",
    )(xp, wall, wall, wall, vec, *traffic.arrays())
    return outs[:4], traffic.split(outs[4:])


def low_lanes(rows):
    return lax.broadcasted_iota(jnp.int32, (rows, LANES), 1) < HEAD


def keys_mask(st):
    tail = st[MAIN:PAD]
    row = lax.broadcasted_iota(jnp.int32, tail.shape, 0)
    return jnp.concatenate([st[:MAIN], jnp.where(row < SEQ - MAIN, tail, NEG)], axis=0)


def diag_mask(heads):
    shape = (heads, heads * HEAD)
    row = lax.broadcasted_iota(jnp.int32, shape, 0)
    return lax.broadcasted_iota(jnp.int32, shape, 1) // HEAD == row


def last_by_head(t_ref, dmask, cols=slice(None)):
    last = t_ref[MAIN:PAD, cols][:1]
    return jnp.where(dmask, jnp.broadcast_to(last.astype(F32), dmask.shape), 0.0).astype(BF16)


def only_first_row(t):
    row = lax.broadcasted_iota(jnp.int32, (TAIL, t.shape[1]), 0)
    return jnp.where(row == 0, jnp.broadcast_to(t, row.shape), 0.0)


def softmax_t(st):
    st = keys_mask(st)
    m = jnp.max(st, axis=0, keepdims=True) * (SCALE * LOG2E)
    e = jnp.exp2(st * (SCALE * LOG2E) - m)
    total = col_sum(e)
    return e, total, m


def two_heads(t, low):
    zero = jnp.zeros(t.shape, t.dtype)
    return jnp.where(low, t, zero), jnp.where(low, zero, t)


def attn_fwd_kernel(traffic, q_ref, k_ref, v_ref, x_ref, g_ref, wo_ref, vec_ref, *refs):
    n_in, n_out, _ = traffic.sizes()
    srcs, (o_ref, a_ref, y_ref, h2_ref, dm_ref, lse_ref, *refs) = refs[:n_in], refs[n_in:]
    dsts, (s_s, p_s, *rest) = refs[:n_out], refs[n_out:]
    i = pl.program_id(0)
    traffic.begin(i, srcs, dsts, rest)
    low_q = low_lanes(MAIN)
    for p in range(HEADS // 2):
        halves = two_heads(q_ref[:MAIN, block(p)], low_q)
        for hh, qa in enumerate(halves):
            s_s[2 * p + hh] = dot_nt(k_ref[:, block(p)], qa)

    @pl.loop(0, ONCE)
    def _(t):
        for h in range(HEADS):
            e, total, m = softmax_t(s_s[h])
            p_s[h] = (e * (1.0 / total)).astype(BF16)
            lse_ref[h:h + 1, :] = m + jnp.log(total) * LOG2E

    for p in range(HEADS // 2):
        vt = v_ref[:, block(p)].T
        outs = [dot_nn(vt[hh * HEAD:(hh + 1) * HEAD], p_s[2 * p + hh]) for hh in range(2)]
        o_ref[:MAIN, block(p)] = jnp.concatenate(outs, axis=0).astype(BF16).T
    dmask = diag_mask(HEADS)
    e, total, _ = softmax_t(dot_nt(k_ref[:], last_by_head(q_ref, dmask)))
    ot = dot_tn((e * (1.0 / total)).astype(BF16), v_ref[:])
    o_ref[MAIN:PAD] = only_first_row(col_sum(jnp.where(dmask, ot, 0.0))).astype(BF16)

    _, _, bo, s1, g2, c2, _, s2 = table_rows(vec_ref)
    a = dot_nn(o_ref[:], wo_ref[:].reshape(D, D)) + bo
    a_ref[:] = a
    y = x_ref[:].astype(F32) + s1 * a
    y_ref[:] = y
    xhat, _ = ln_fwd(y)
    h2_ref[:] = (xhat * g2 + c2).astype(BF16)
    dm_ref[:] = (g_ref[:].astype(F32) * s2).astype(BF16)
    traffic.finish(i == NSEQ - 1)


def run_attn_fwd(q, k, v, xp, gp, wo, vec, cid, items):
    traffic = Traffic(items)
    tok = one_seq()
    outs = pl.pallas_call(
        functools.partial(attn_fwd_kernel, traffic), grid=(NSEQ,),
        in_specs=[tok] * 5 + [wblk(0), fixed(vec.shape)] + traffic.in_specs(),
        out_specs=[tok] * 5 + [pl.BlockSpec((None, HEADS, MAIN), lambda s: (s, 0, 0))] + traffic.out_specs(),
        out_shape=[act(), act(dtype=F32), act(dtype=F32), act(), act(), f32s(NSEQ, HEADS, MAIN)] + traffic.out_shapes(),
        scratch_shapes=[pltpu.VMEM((HEADS, PAD, MAIN), F32), pltpu.VMEM((HEADS, PAD, MAIN), BF16)] + traffic.scratch(),
        input_output_aliases=traffic.aliases(7, 6),
        compiler_params=comm_params(cid), name="attn_fwd",
    )(q, k, v, xp, gp, wo, vec, *traffic.arrays())
    return outs[:6], traffic.split(outs[6:])


def owner_rows(load, core):
    _, y, x, _ = coords()
    pieces = []
    for yy in (y, 1 - y):
        for xx in (x, 1 - x):
            pieces.append(load(pl.ds(pl.multiple_of((4 * yy + 2 * xx + core) * ROWS, ROWS), ROWS)))
    return jnp.concatenate(pieces, axis=1)


def store_piece(ab_ref, mine_ref, came_ref, unit):
    for color in range(2):
        for ry in range(2):
            for rx in range(2):
                r = 2 * ry + rx
                rows = slice(r * ROWS, (r + 1) * ROWS)
                sent, pos = (rx, ry) if color == 0 else (ry, rx)
                ab_ref[color, sent, pos, unit] = mine_ref[color, rows] + came_ref[color, rows]


class CorePair:
    def __init__(self, i, order, part_s, recv_s, sems):
        self.i, self.order, self.part_s, self.recv_s = i, order, part_s, recv_s
        self.slots = part_s.shape[0]
        self.sends = [[Move(remote(part_s.at[u % self.slots, n], recv_s.at[u, n], sems, 2 * u + n, partner("core")))
                       for n in range(2)] for u in range(recv_s.shape[0])]

    def before(self):
        for step, (what, u) in self.order.items():
            @pl.when(self.i == step)
            def _(step=step, what=what, u=u):
                came, prev = self.order.get(step - 1, ("none", 0))
                if came == "part":
                    self.sends[prev][1].start()
                if what == "mine":
                    for mv in self.sends[u]:
                        mv.sent()

    def product(self, u, left, right):
        theirs, mine = [next(st for st, which in self.order.items() if which == (what, u)) for what in ("part", "mine")]
        core = lax.rem(lax.axis_index("fsdp"), 2)

        @pl.when((self.i == theirs) | (self.i == mine))
        def _():
            who = jnp.where(self.i == mine, core, 1 - core)

            @pl.loop(0, 2)
            def _(n):
                @pl.when((self.i == theirs) & (n == 1))
                def _():
                    self.sends[u][0].start()
                cols = pl.ds(pl.multiple_of(n * HD, HD), HD)
                self.part_s[u % self.slots, n] = dot_tn(owner_rows(left, who), right(cols))

    def after(self, ab_ref, unit_of):
        for step, (what, u) in self.order.items():
            if what == "mine":
                @pl.when(self.i == step)
                def _(u=u):
                    for mv in self.sends[u]:
                        mv.recv()
                    store_piece(ab_ref, self.part_s.at[u % self.slots], self.recv_s.at[u], unit_of(u))


def pair_scratch(n):
    half = (2, 4 * ROWS, HD)
    return [pltpu.VMEM((2,) + half, F32), pltpu.VMEM((n,) + half, F32),
            pltpu.SemaphoreType.DMA((2 * n,)), pltpu.SemaphoreType.DMA((2 * n,))]


def piece_spec(width, n, before):
    return pl.BlockSpec((2, 2, 2, 1, ROWS, width // 2),
                        lambda i: (0, 0, 0, jnp.clip(i - before, 0, n - 1), 0, 0))


def mlp_kernel(first, traffic, h2_any, dm_any, wff_any, b1_ref, *refs):
    n_in, n_out, _ = traffic.sizes()
    if not first:
        m_in, dh_in, *refs = refs
    srcs, (m_out, dh_out, ab_ref, db_ref, *refs) = refs[:n_in], refs[n_in:]
    dsts, (h2_ref, dm_ref, w_s, load_sem, act_s, du_s, part_s, recv_s, core_send, core_recv, *rest) = refs[:n_out], refs[n_out:]
    i = pl.program_id(0)
    bs = m_out.shape[0]
    rows = bs * PAD
    nblk = NSEQ // bs
    traffic.begin(i, srcs, dsts, rest)

    loads = [pltpu.make_async_copy(wff_any.at[:, block(k)], w_s.at[k], load_sem.at[k]) for k in range(2)]
    w1_load, w2_load = loads

    def blocks(j):
        some = pl.ds(j * bs, bs)
        return [pltpu.make_async_copy(src.at[some], dst.at[some], load_sem.at[2 + 2 * j + k])
                for k, (src, dst) in enumerate(((h2_any, h2_ref), (dm_any, dm_ref)))]

    @pl.when(i == 0)
    def _():
        db_ref[:] = jnp.zeros_like(db_ref)
        h2_load, dm_load = blocks(0)
        for cp in (w1_load, h2_load, w2_load, dm_load):
            cp.start()
        for j in range(1, nblk):
            for cp in blocks(j):
                cp.start()

    for j in range(nblk):
        @pl.when(i == j)
        def _(j=j):
            for cp in blocks(j) + ([] if j else loads):
                cp.wait()

    @pl.when(i < nblk)
    def _():
        hb = h2_ref[pl.ds(i * bs, bs)].reshape(rows, D)
        dmb = dm_ref[pl.ds(i * bs, bs)].reshape(rows, D)
        w1 = w_s[0].reshape(D, QTR)
        w2 = w_s[1].reshape(QTR, D)
        mine = pl.ds(pl.multiple_of(i * rows, rows), rows)
        cw = 2 * LANES
        for c in range(QTR // cw):
            cols = slice(c * cw, (c + 1) * cw)
            u = dot_nn(hb, w1[:, cols]) + b1_ref[:, cols]
            da = dot_nt(dmb, w2[cols])
            cdf = 0.5 + 0.5 * lax.erf(u * (0.5 ** 0.5))
            slope = cdf + u * (jnp.exp(-0.5 * u * u) * 0.3989422804014327)
            du = da * slope
            db_ref[:, cols] += sub8(du)
            act_s[mine, cols] = (u * cdf).astype(BF16)
            du_s[mine, cols] = du.astype(BF16)
        m = dot_nn(act_s[mine, :], w2).reshape(m_out.shape)
        dh = dot_nt(du_s[mine, :], w1).reshape(dh_out.shape)
        m_out[:] = m if first else m_in[:] + m
        dh_out[:] = dh if first else dh_in[:] + dh

    flat = NSEQ * PAD
    order = {nblk + 2 * k + u: (what, u) for k, what in enumerate(("part", "mine")) for u in range(2)}
    pair = CorePair(i, order, part_s, recv_s, (core_send, core_recv))
    pair.before()
    pair.product(0, lambda lanes: h2_ref[:, :, lanes].reshape(flat, ROWS), lambda cols: du_s[:, cols])
    pair.product(1, lambda lanes: act_s[:, lanes], lambda cols: dm_ref[:, :, cols].reshape(flat, cols.size))
    pair.after(ab_ref, lambda u: 0)
    traffic.finish(i == pl.num_programs(0) - 1)


def run_mlp(h2, dm, wff, b1, acc, cid, items=()):
    traffic = Traffic(items, ("core",))
    bs = 2
    nblk = NSEQ // bs
    tok = pl.BlockSpec((bs, PAD, D), lambda i: (jnp.minimum(i, nblk - 1), 0, 0))
    args = (h2, dm, wff, b1) + acc
    base = len(args)
    outs = pl.pallas_call(
        functools.partial(mlp_kernel, not acc, traffic), grid=(nblk + 4,),
        in_specs=[ANY] * 3 + [fixed(b1.shape)] + [tok] * len(acc) + traffic.in_specs(),
        out_specs=[tok, tok, piece_spec(D, 2, nblk + 2), resident((8, QTR))] + traffic.out_specs(),
        out_shape=[act(dtype=F32), act(dtype=F32), f32s(2, 2, 2, 2, ROWS, HD), f32s(8, QTR)] + traffic.out_shapes(),
        scratch_shapes=[pltpu.VMEM(h2.shape, BF16), pltpu.VMEM(dm.shape, BF16), pltpu.VMEM((2, PEERS, ROWS, D), BF16),
                        pltpu.SemaphoreType.DMA((2 + 2 * nblk,))] + [pltpu.VMEM((NSEQ * PAD, QTR), BF16)] * 2
        + pair_scratch(2) + traffic.scratch(),
        input_output_aliases={**{base - len(acc) + k: k for k in range(len(acc))}, **traffic.aliases(base, 4)},
        compiler_params=comm_params(cid), name="mlp",
    )(*args, *traffic.arrays())
    m, dh, ab, db, *rest = outs
    return (m, dh), ab, db, traffic.split(rest)


ORDER = ("part0", "part1", "mine0", "part2", "mine1", "part3", "mine2", "mine3")
EARLY = 2
LOADED = ("o", "da", "h1", "dv", "dk", "dq")
LOADED_AT = ("o da", "h1 dv", "", "dk", "", "dq")


def wgrad_kernel(traffic, *refs):
    given, refs = refs[:len(LOADED)], refs[len(LOADED):]
    n_in, n_out, _ = traffic.sizes()
    srcs, (ab_ref, *refs) = refs[:n_in], refs[n_in:]
    early, refs = refs[:EARLY], refs[EARLY:]
    dsts, refs = refs[:n_out], refs[n_out:]
    here, refs = refs[:len(LOADED)], refs[len(LOADED):]
    load_sem, part_s, recv_s, core_send, core_recv, s1_send, s1_recv, *rest = refs
    i = pl.program_id(0)
    flat = NSEQ * PAD
    traffic.begin(i, srcs, dsts, rest)
    loads = [pltpu.make_async_copy(src, dst, load_sem.at[k]) for k, (src, dst) in enumerate(zip(given, here))]

    @pl.when(i == 0)
    def _():
        for cp in loads:
            cp.start()

    for step, some in enumerate(LOADED_AT):
        @pl.when(i == step)
        def _(some=some):
            for name in some.split():
                loads[LOADED.index(name)].wait()

    o, da, h1, dv, dk, dq = here
    units = ((o, da), (h1, dv), (h1, dk), (h1, dq))
    onward = [[Move(remote(ab_ref.at[color, 1, :, u], got.at[color], (s1_send, s1_recv), 2 * u + color, partner(nm)))
               for color, nm in enumerate(NAMES["s1"])] for u, got in enumerate(early)]
    order = {step: (name[:DEPTH], int(name[DEPTH:])) for step, name in enumerate(ORDER)}
    pair = CorePair(i, order, part_s, recv_s, (core_send, core_recv))
    pair.before()
    for step, (what, u) in order.items():
        if what == "mine" and u < EARLY:
            @pl.when(i == step + 1)
            def _(u=u):
                for mv in onward[u]:
                    mv.start()
    for u, (left, right) in enumerate(units):
        pair.product(u, lambda lanes, left=left: left[:, :, lanes].reshape(flat, ROWS),
                     lambda cols, right=right: right[:, :, cols].reshape(flat, cols.size))
    pair.after(ab_ref, lambda u: u)

    @pl.when(i == len(ORDER) - 1)
    def _():
        for moves in onward:
            for mv in moves:
                mv.recv()
                mv.sent()

    traffic.finish(i == len(ORDER) - 1)


def run_wgrad(ops, cid, items):
    traffic = Traffic(items, ("core", "x", "y"))
    n = DEPTH
    piece = (2, 2, 2, n, ROWS, HD)
    dma = pltpu.SemaphoreType.DMA
    outs = pl.pallas_call(
        functools.partial(wgrad_kernel, traffic), grid=(len(ORDER),),
        in_specs=[ANY] * len(ops) + traffic.in_specs(),
        out_specs=[fixed(piece)] + [ANY] * EARLY + traffic.out_specs(),
        out_shape=[f32s(*piece)] + [f32s(2, 2, ROWS, HD)] * EARLY + traffic.out_shapes(),
        scratch_shapes=[pltpu.VMEM(t.shape, BF16) for t in ops] + [dma((len(ops),))] + pair_scratch(n)
        + [dma((2 * EARLY,)), dma((2 * EARLY,))] + traffic.scratch(),
        input_output_aliases=traffic.aliases(len(ops), 1 + EARLY),
        compiler_params=comm_params(cid), name="wgrad",
    )(*ops, *traffic.arrays())
    ab, *outs = outs
    return ab, outs[:EARLY], traffic.split(outs[EARLY:])


def heads_bwd(half, q_ref, k_ref, v_ref, do_ref, lse_ref, dq_ref, dk_ref, dv_ref, sum_ref,
              dk_s, dv_s, s_s, dp_s, p_s, ds_s):
    low_q, low_k = low_lanes(MAIN), low_lanes(PAD)
    pairs = HH // 2
    cols = slice(half * HD, (half + 1) * HD)
    for p in range(pairs):
        lanes = block(half * pairs + p)
        queries = two_heads(q_ref[:MAIN, lanes], low_q)
        cots = two_heads(do_ref[:MAIN, lanes], low_q)
        for hh in range(2):
            s_s[2 * p + hh] = dot_nt(k_ref[:, lanes], queries[hh])
            dp_s[2 * p + hh] = dot_nt(v_ref[:, lanes], cots[hh])

    @pl.loop(0, ONCE)
    def _(t):
        for h in range(HH):
            dpt = dp_s[h]
            lse = lse_ref[half * HH + h:half * HH + h + 1, :]
            prob = jnp.exp2(keys_mask(s_s[h]) * (SCALE * LOG2E) - lse)
            p_s[h] = prob.astype(BF16)
            ds_s[h] = (prob * (dpt - col_sum(prob * dpt)) * SCALE).astype(BF16)

    dmask = diag_mask(HH)
    qb, dob = last_by_head(q_ref, dmask, cols), last_by_head(do_ref, dmask, cols)
    e, total, _ = softmax_t(dot_nt(k_ref[:, cols], qb))
    prob = e * (1.0 / total)
    dp = dot_nt(v_ref[:, cols], dob)
    ds = (prob * (dp - col_sum(prob * dp)) * SCALE).astype(BF16)
    dv_s[:] = dot_nn(prob.astype(BF16), dob)
    dk_s[:] = dot_nn(ds, qb)
    dq_tail = only_first_row(col_sum(jnp.where(dmask, dot_tn(ds, k_ref[:, cols]), 0.0)))
    dq_ref[MAIN:PAD, cols] = dq_tail.astype(BF16)
    sum_ref[0, :, cols] += sub8(dq_tail)

    for p in range(pairs):
        lanes = block(half * pairs + p)
        q2, do2 = q_ref[:MAIN, lanes], do_ref[:MAIN, lanes]
        kt = k_ref[:, lanes].T
        heads = range(2 * p, 2 * p + 2)
        dv = jnp.where(low_k, *[dot_nn(p_s[h], do2) for h in heads]) + dv_s[:, block(p)]
        dk = jnp.where(low_k, *[dot_nn(ds_s[h], q2) for h in heads]) + dk_s[:, block(p)]
        dq = jnp.concatenate([dot_nn(kt[hh * HEAD:(hh + 1) * HEAD], ds_s[h]) for hh, h in enumerate(heads)], axis=0).T
        dv_ref[:, lanes] = dv.astype(BF16)
        dk_ref[:, lanes] = dk.astype(BF16)
        dq_ref[:MAIN, lanes] = dq.astype(BF16)
        for k, t in enumerate((dq, dk, dv)):
            sum_ref[k, :, lanes] += sub8(t)


def heads_scratch():
    scores = (HH, PAD, MAIN)
    return [pltpu.VMEM((PAD, HD), F32), pltpu.VMEM((PAD, HD), F32), pltpu.VMEM(scores, F32), pltpu.VMEM(scores, F32),
            pltpu.VMEM(scores, BF16), pltpu.VMEM(scores, BF16)]


def back_kernel(traffic, m_ref, y_ref, dh_ref, a_ref, g_ref, q_ref, k_ref, v_ref, lse_ref, wo_ref, vec_ref, *refs):
    n_in, n_out, _ = traffic.sizes()
    srcs, (z_ref, gres_ref, da_ref, dq_ref, dk_ref, dv_ref, sum_ref, hsum_ref, *refs) = refs[:n_in], refs[n_in:]
    dsts, (do_s, *refs) = refs[:n_out], refs[n_out:]
    n = len(heads_scratch())
    heads = refs[:n]
    i = pl.program_id(0)
    traffic.begin(i, srcs, dsts, refs[n:])

    @pl.when(i == 0)
    def _():
        sum_ref[:] = jnp.zeros_like(sum_ref)
        hsum_ref[:] = jnp.zeros_like(hsum_ref)

    _, _, _, s1, g2, _, b2, s2 = table_rows(vec_ref)
    g = g_ref[:].astype(F32)
    y = y_ref[:]
    m = m_ref[:] + b2
    z_ref[:] = (y + s2 * m).astype(BF16)[:SEQ]
    dh = dh_ref[:]
    xhat, rstd = ln_fwd(y)
    gres = g + ln_bwd(dh * g2, xhat, rstd)
    gres_ref[:] = gres
    da = gres * s1
    for k, t in enumerate((da, gres * a_ref[:], dh * xhat, dh, g * s2, g * m)):
        sum_ref[k] += sub8(t)
    dab = da.astype(BF16)
    da_ref[:] = dab
    do_s[:] = dot_nt(dab, wo_ref[:].reshape(D, D)).astype(BF16)
    for half in range(2):
        heads_bwd(half, q_ref, k_ref, v_ref, do_s, lse_ref, dq_ref, dk_ref, dv_ref, hsum_ref, *heads)
    traffic.finish(i == NSEQ - 1)


def run_back(m, y, dh, a, gp, q, k, v, lse, wo, vec, cid, items):
    traffic = Traffic(items)
    tok = one_seq()
    outs = pl.pallas_call(
        functools.partial(back_kernel, traffic), grid=(NSEQ,),
        in_specs=[tok] * 8 + [pl.BlockSpec((None, HEADS, MAIN), lambda s: (s, 0, 0)), wblk(0), fixed(vec.shape)]
        + traffic.in_specs(),
        out_specs=[pl.BlockSpec((None, SEQ, D), lambda s: (s, 0, 0))] + [tok] * 5
        + [resident((6, 8, D)), resident((3, 8, D))] + traffic.out_specs(),
        out_shape=[jax.ShapeDtypeStruct((NSEQ, SEQ, D), BF16), act(dtype=F32)] + [act()] * 4
        + [f32s(6, 8, D), f32s(3, 8, D)] + traffic.out_shapes(),
        scratch_shapes=[pltpu.VMEM((PAD, D), BF16)] + heads_scratch() + traffic.scratch(),
        input_output_aliases=traffic.aliases(11, 8),
        compiler_params=comm_params(cid), name="back",
    )(m, y, dh, a, gp, q, k, v, lse, wo, vec, *traffic.arrays())
    return outs[:8], traffic.split(outs[8:])


def adds_kernel(n, *refs):
    ins, outs = refs[:2 * n], refs[2 * n:]
    for a_ref, b_ref, o_ref in zip(ins[::2], ins[1::2], outs):
        o_ref[:] = a_ref[:].reshape(o_ref.shape) + b_ref[:].reshape(o_ref.shape)


def quarters(shape, kept=False):
    *lead, rows, width = shape
    lead = (1,) + ((1,) + tuple(lead[2:]) if kept else tuple(lead[1:]))
    zeros = (0,) * (len(lead) - 1)
    return pl.BlockSpec(lead + (rows // 2, width), lambda g: (g // 2,) + zeros + (lax.rem(g, 2), 0))


def run_adds(*jobs):
    specs, outs = [], []
    for a, b in jobs:
        outs.append(quarters(b.shape))
        specs += [quarters(a.shape, a.ndim > b.ndim), outs[-1]]
    return pl.pallas_call(
        functools.partial(adds_kernel, len(jobs)), grid=(4,), in_specs=specs, out_specs=outs,
        out_shape=[f32s(*b.shape) for _, b in jobs],
        compiler_params=params(), name="adds",
    )(*[t for job in jobs for t in job])


def store_ff(gup_ref, gdown_ref, f_ref, j):
    half = PEERS // 2
    for k in range(PEERS):
        gup_ref[:, block(DEPTH * k + j)] = f_ref[k // half, 0, :, block(k % half)]
    for color in range(2):
        gdown_ref[j * ROWS:(j + 1) * ROWS, color * HD:(color + 1) * HD] = f_ref[color, 1]


UNITS = DEPTH
EVENTS = ("", "", "b0", "b1", "p00", "p01", "a2 p10 q00", "p11 q01")


def finish_kernel(x_ref, gres_ref, dq_ref, dk_ref, dv_ref, wq_ref, wk_ref, wv_ref, vec_ref, ab_any, keep_ref, e0, e1,
                  f0, f1, f2, p3_ref, b3_ref, sum_ref, hsum_ref, db0, db1, db2, db3,
                  dx_ref, gqkv_ref, gout_ref, gup_ref, gdown_ref, small_ref,
                  dx_s, ln_s, sk, r2, ra, rb, f3_s, small_s, all_p, part_s, all_z, ssem, rsem):
    i = pl.program_id(0)
    z, me = lax.axis_index("rep"), lax.axis_index("fsdp")
    sems, used = (ssem, rsem), []
    colors = range(2)

    def move(src, dst, device, *roles):
        used.append(Move(remote(src, dst, sems, len(used), device), *roles))
        return used[-1]

    s1 = {u: [move(ab_any.at[color, 1, :, u], sk.at[u, color], partner(nm)) for color, nm in enumerate(NAMES["s1"])]
          for u in range(EARLY, UNITS)}
    s2 = [[move(sk.at[u, color, 1], r2.at[u, color], partner(nm)) for color, nm in enumerate(NAMES["s2"])]
          for u in range(UNITS)]
    near, far = partner("near"), partner("far")
    z_a = [[move(sk.at[u, c, 0], ra.at[u, c], near, *ROLES["zA"]) for c in colors] for u in range(UNITS)]
    z_b = [[move(ra.at[u, c], rb.at[u, c], far, *ROLES["zB"]) for c in colors] for u in range(UNITS)]
    z_c = [[move(rb.at[u, c], rb.at[u, c], near, *ROLES["zC"]) for c in colors] for u in range(UNITS)]
    f3_c = move(f3_s, f3_s, near, *ROLES["zC"])
    others = [(z, lax.rem(me + k, PEERS)) for k in range(1, PEERS)]
    column = [(lax.rem(z + k, DEPTH), me) for k in range(1, DEPTH)]
    plane_moves = [move(small_s.at[to], all_p.at[me], (zz, to)) for zz, to in others]
    column_moves = [move(part_s, all_z.at[z], dev) for dev in column]

    def start(moves):
        for mv in moves:
            mv.start()

    def arrive(moves):
        for mv in moves:
            mv.recv()

    def inner(do):
        pl.when(is_inner() == 1)(do)

    def after_s1(u, came=None):
        if came is None:
            arrive(s1[u])
        for pos in (1, 0):
            for c in colors:
                got = sk[u, c, pos] if came is None else came[c, pos]
                sk[u, c, pos] = got + keep_ref[c, 0, pos, u]
        start(s2[u])

    def after_s2(u):
        arrive(s2[u])
        for c in colors:
            sk[u, c, 0] = sk[u, c, 0] + r2[u, c]
        start(z_a[u])

    def after_za(u, c):
        arrive([z_a[u][c]])

        @inner
        def _():
            ra[u, c] = ra[u, c] + sk[u, c, 0]
        start([z_b[u][c]])

    def after_zb(u, c):
        arrive([z_b[u][c]])

        @inner
        def _():
            rb[u, c] = rb[u, c] + ra[u, c]
        start([z_c[u][c]])

    @pl.when(i == 0)
    def _():
        greet(others + column)
        ln_s[:] = jnp.zeros_like(ln_s)

        @inner
        def _():
            f3_s[:] = p3_ref[:] + b3_ref[:]
        start([f3_c])
        for u, came in enumerate((e0, e1)):
            after_s1(u, came)
        for u in s1:
            start(s1[u])

    act_on = {"a": after_s1, "b": after_s2, "p": after_za, "q": after_zb}

    def handle(events):
        for kind, *which in events.split():
            act_on[kind](*map(int, which))

    for step, events in enumerate(EVENTS):
        @pl.when(i == step)
        def _(events=events):
            handle(events)

    dh = None
    for d_ref, w_ref in ((dq_ref, wq_ref), (dk_ref, wk_ref), (dv_ref, wv_ref)):
        part = dot_nt(d_ref[:], w_ref[:].reshape(D, D))
        dh = part if dh is None else dh + part
    g1, *_ = table_rows(vec_ref)
    xhat, rstd = ln_fwd(x_ref[:].astype(F32))
    for k, t in enumerate((dh * xhat, dh)):
        ln_s[k] += sub8(t)
    dx = gres_ref[:] + ln_bwd(dh * g1, xhat, rstd)
    for k in range(PEERS):
        dx_s[k, pl.ds(i, SEQ, stride=NSEQ), :] = dx[:SEQ, block(k)]

    @pl.when(i == NSEQ - 1)
    def _():
        rows = [col_sum(ref[k]) for ref in (ln_s, sum_ref) for k in range(ref.shape[0])]
        rows += [col_sum(ref[:]) for ref in (db0, db1, db2, db3)]
        blocks = [col_sum(hsum_ref[t])[:, block(k)] for t in range(3) for k in range(PEERS)]
        for to in range(PEERS):
            mine = [row[:, block(to)] for row in rows] + blocks[3 * to:3 * to + 3] + [jnp.zeros((1, LANES), F32)]
            small_s[to] = jnp.concatenate(mine, axis=0)
        start(plane_moves)
        all_p[me] = small_s[me]
        handle("a3")
        for k in range(PEERS):
            dx_ref[:, :, block(k)] = dx_s[k].reshape(SEQ, NSEQ, LANES).astype(BF16)
        handle("q10")
        arrive(plane_moves)
        part_s[:] = jnp.sum(all_p[:], axis=0)
        all_z[z] = part_s[:]
        start(column_moves)
        handle("b2 q11")
        for j, f_ref in enumerate((f0, f1, f2)):
            store_ff(gup_ref, gdown_ref, f_ref, j)
        handle("b3 p20")
        arrive([f3_c])
        store_ff(gup_ref, gdown_ref, f3_s, 3)
        arrive(column_moves)
        small_ref[:] = jnp.sum(all_z[:], axis=0)
        handle("p21 q20 p30")
        handle("q21 p31 q30 q31")
        for u, (out_ref, base) in enumerate(((gout_ref, 0), (gqkv_ref, 2 * D), (gqkv_ref, D), (gqkv_ref, 0))):
            for c in colors:
                arrive(z_c[u][c:c + 1])
                out_ref[:, base + c * HD:base + (c + 1) * HD] = rb[u, c]
        for mv in used:
            mv.sent()


def run_finish(xp, gres, grads, wall, vec, ab, early, ffs, last, sums, hsum, dbs, cid):
    tok = one_seq()
    outs = [(SEQ, NSEQ, D), (ROWS, 3 * D), (ROWS, D), (ROWS, DEPTH * D), (DEPTH * ROWS, D), (16, LANES)]

    def piece(*lead):
        return pltpu.VMEM(lead + (ROWS, HD), F32)

    scratch = [pltpu.VMEM((PEERS, SEQ * NSEQ, LANES), F32), pltpu.VMEM((2, 8, D), F32)]
    scratch += [piece(UNITS, 2, 2)] + [piece(UNITS, 2)] * 3 + [piece(2, 2)]
    scratch += [pltpu.VMEM((PEERS, 16, LANES), F32)] * 2
    scratch += [pltpu.VMEM((16, LANES), F32), pltpu.VMEM((DEPTH, 16, LANES), F32)]
    scratch += [pltpu.SemaphoreType.DMA((64,)), pltpu.SemaphoreType.DMA((64,))]
    consts = [sums, hsum] + list(dbs)
    held = [*early, *ffs, *last]
    before = [xp, gres, *grads, wall, wall, wall, vec, ab, ab, *held]
    return pl.pallas_call(
        finish_kernel, grid=(NSEQ,),
        in_specs=[tok] * 5 + [*map(wblk, range(3)), fixed(vec.shape), ANY, kept_spec(ab.shape)]
        + [fixed(t.shape) for t in held + consts],
        out_specs=[fixed(sh) for sh in outs],
        out_shape=[jax.ShapeDtypeStruct(outs[0], BF16)] + [f32s(*sh) for sh in outs[1:]],
        scratch_shapes=scratch, compiler_params=comm_params(cid), name="finish",
    )(*before, *consts)


def device_step(x_loc, dz_loc, w_qkv, b_qkv, w_out, w_up, b_up, w_down, vec_params):
    cid = itertools.count()
    vecs = jnp.concatenate([vec_params, b_up.reshape(-1, LANES), b_qkv.reshape(-1, LANES), jnp.zeros((1, LANES), F32)])
    xp, gp, wall, wo, c0, c1, c2, c3, vec = run_intake(
        x_loc.swapaxes(0, 1), dz_loc.swapaxes(0, 1), w_qkv, w_out, w_up, w_down, vecs, next(cid))
    b1 = [vec[V_UP + j:V_UP + j + 1] for j in range(DEPTH)]
    own, rest = range(2)
    (h1, q, k, v), (wo,) = run_qkv(xp, wall, vec, next(cid), [Gather(wo, own, 2, 3)])
    (o, a, y, h2, dm, lse), (c0, c1) = run_attn_fwd(
        q, k, v, xp, gp, wo, vec, next(cid), [Gather(c0, own, 3, 5), Gather(c1, own, start=3)])

    mlp = functools.partial(run_mlp, h2, dm)
    acc, f0, db0, (c1, c2, c3) = mlp(c0, b1[0], (), next(cid), [Gather(c1, rest, 3), Gather(c2, own), Gather(c3, own)])
    acc, f1, db1, (c2, c3, r0) = mlp(
        c1, b1[1], acc, next(cid), [Gather(c2, rest, 3), Gather(c3, rest, 4), Chain(f0, "s1")])
    f0, = run_adds((f0, r0))
    acc, f2, db2, (r0, r1) = mlp(c2, b1[2], acc, next(cid), [Chain(f0, "s2", ("zA", 2)), Chain(f1, "s1")])
    f1, f0 = run_adds((f1, r1), r0)
    acc, f3, db3, (r1, r2, r0) = mlp(
        c3, b1[3], acc, next(cid), [Chain(f1, "s2", ("zA", 2)), Chain(f2, "s1"), Chain(f0, "zB")])
    f2, f1, f0 = run_adds((f2, r2), r1, (f0, r0))
    m, dh = acc
    (z, gres, da, dq, dk, dv, sums, hsum), (r2, r3, f1, f0) = run_back(
        m, y, dh, a, gp, q, k, v, lse, wo, vec, next(cid),
        [Chain(f2, "s2", ("zA", 2), ("zB", 4, 5)), Chain(f3, "s1", ("s2", 5)), Chain(f1, "zB", ("zC", 2, 4)), Chain(f0, "zC")])
    f3, f2 = run_adds(r3, r2)
    ab, early, (r3, f2) = run_wgrad([o, da, h1, dv, dk, dq], next(cid), [Chain(f3, "zA", ("zB", 4, 7)), Chain(f2, "zC")])
    dx, g_qkv, g_out, g_up, g_down, small = run_finish(
        xp, gres, [dq, dk, dv], wall, vec, ab, early, [f0, f1, f2], r3, sums, hsum, [db0, db1, db2, db3], next(cid))
    g_bup, g_bqkv = small[V_UP:V_QKV].reshape(-1), small[V_QKV:V_QKV + 3].reshape(-1)
    return z, dx.swapaxes(0, 1), g_qkv, g_bqkv, g_out, g_up, g_bup, g_down, small[:V_UP]


def solution(mesh):
    batch = P(("rep", "fsdp"), None, None)
    row, flat, col = P("fsdp", None), P("fsdp"), P(None, "fsdp")
    par = (row, flat, row, row, flat, row, col)
    return jax.shard_map(device_step, mesh=mesh, in_specs=(batch, batch) + par,
                         out_specs=(batch, batch) + par, check_vma=False)
```

profile of v0, /device:TPU:0, one launch (start us, length us, event | category | flops | bytes accessed | tf_op | source)
XLA Modules:
  0.0 526.6 jit_solution(10269810710824034719)
XLA Ops:
  0.6 0.1 pad.3.clone
  0.7 1.4 maximum_maximum_fusion.vecs
  2.1 37.6 %intake.1 = (bf16[8,272,1024]{2,1,0:T(8,128)(2,1)}, bf16[8,272,1024]{2,1,0:T(8,128)(2,1)}, bf16[8,384,1024]{2,1,0:T(8,128)(2,1)}, bf16[8,128,1024]{2,1,0:T(8,128...) custom-call(bf16[257,8,1024]{2,1,0:T(8,128)(2,1)} %bitcast.10, ...), custom_call_target="tpu_custom_call" | custom-call | tf_op jit(solution)/shard_map/intake/pallas_call | solution.py:505
  39.7 1.5 fusion
  41.2 23.8 %qkv.1 = (bf16[8,272,1024]{2,1,0:T(8,128)(2,1)}, bf16[8,272,1024]{2,1,0:T(8,128)(2,1)}, bf16[8,272,1024]{2,1,0:T(8,128)(2,1)}, bf16[8,272,1024]{2,1,0:T(8,128)(2,1)}, bf16[8,128,1024]{2,1,0:T(8,128)(2,1)}) custom-call(bf16[8,272,1024]{2,1,0:T(8,128)(2,1)} %get-tuple-element.93.x_ref, ...), custom_call_target="tpu_custom_call", output_to_operand_aliasing={{4}: (5, {})} | custom-call | tf_op jit(solution)/shard_map/qkv/pallas_call | solution.py:540
  65.1 38.8 %attn_fwd.1 = (bf16[8,272,1024]{2,1,0:T(8,128)(2,1)}, f32[8,272,1024]{2,1,0:T(8,128)}, f32[8,272,1024]{2,1,0:T(8,128)}, bf16[8,272,1024]{2,1,0:T(8,128)(2,1)}, b...) custom-call(bf16[8,272,1024]{2,1,0:T(8,128)(2,1)} %get-tuple-element, ...), custom_call_target="tpu_custom_call", output_to_operand_aliasing={{6}: (7, {}), {7}: (8, {})} | custom-call | tf_op jit(solution)/shard_map/attn_fwd/pallas_call | solution.py:631
  103.9 42.0 %mlp.4 = (f32[8,272,1024]{2,1,0:T(8,128)}, f32[8,272,1024]{2,1,0:T(8,128)}, f32[2,2,2,2,128,512]{5,4,3,2,1,0:T(8,128)}, f32[8,1024]{1,0:T(8,128)}, bf16[8,256,10...) custom-call(bf16[8,272,1024]{2,1,0:T(8,128)(2,1)} %get-tuple-element, ...), custom_call_target="tpu_custom_call", output_to_operand_aliasing={{4}: (4, {}), {5}: (5, {}), {6}: (6, {})} | custom-call | tf_op jit(solution)/shard_map/mlp/pallas_call | solution.py:793
  145.9 43.7 %mlp.5 = (f32[8,272,1024]{2,1,0:T(8,128)}, f32[8,272,1024]{2,1,0:T(8,128)}, f32[2,2,2,2,128,512]{5,4,3,2,1,0:T(8,128)}, f32[8,1024]{1,0:T(8,128)}, bf16[8,256,10...) custom-call(bf16[8,272,1024]{2,1,0:T(8,128)(2,1)} %get-tuple-element, ...), custom_call_target="tpu_custom_call", output_to_operand_aliasing={{0}: (4, {}), {1}: (5, {}), {4}: (6, {}), {5}: (7, {})} | custom-call | tf_op jit(solution)/shard_map/mlp/pallas_call | solution.py:793
  189.7 4.2 adds.4.refs_2_.refs_3_
  193.9 45.4 %mlp.6 = (f32[8,272,1024]{2,1,0:T(8,128)}, f32[8,272,1024]{2,1,0:T(8,128)}, f32[2,2,2,2,128,512]{5,4,3,2,1,0:T(8,128)}, f32[8,1024]{1,0:T(8,128)}, f32[2,2,128,5...) custom-call(bf16[8,272,1024]{2,1,0:T(8,128)(2,1)} %get-tuple-element, ...), custom_call_target="tpu_custom_call", output_to_operand_aliasing={{0}: (4, {}), {1}: (5, {})} | custom-call | tf_op jit(solution)/shard_map/mlp/pallas_call | solution.py:793
  239.3 4.9 adds.5
  244.2 44.4 %mlp.7 = (f32[8,272,1024]{2,1,0:T(8,128)}, f32[8,272,1024]{2,1,0:T(8,128)}, f32[2,2,2,2,128,512]{5,4,3,2,1,0:T(8,128)}, f32[8,1024]{1,0:T(8,128)}, f32[2,2,128,5...) custom-call(bf16[8,272,1024]{2,1,0:T(8,128)(2,1)} %get-tuple-element, ...), custom_call_target="tpu_custom_call", output_to_operand_aliasing={{0}: (4, {}), {1}: (5, {})} | custom-call | tf_op jit(solution)/shard_map/mlp/pallas_call | solution.py:793
  288.6 5.7 %adds.6 = (f32[2,2,2,128,512]{4,3,2,1,0:T(8,128)}, f32[2,2,128,512]{3,2,1,0:T(8,128)}, f32[2,2,128,512]{3,2,1,0:T(8,128)}) custom-call(f32[2,2,2,2,128,512]{5,4,3,2,1,0:T(8,128)} %get-tuple-element.128.refs_4_.refs_0_, f32[2,2,2,128,512]{4,3,2,1,0:T(8,128)} %get-tuple-element.135.refs_1_, f32[2,2,128,512]{3,2,1,0:T(8,128)} %get-tuple-element.136.refs_2_, ...), custom_call_target="tpu_custom_call" | custom-call | tf_op jit(solution)/shard_map/adds/pallas_call | solution.py:1010
  294.3 64.9 %back.1 = (bf16[8,257,1024]{2,1,0:T(8,128)(2,1)}, f32[8,272,1024]{2,1,0:T(8,128)}, bf16[8,272,1024]{2,1,0:T(8,128)(2,1)}, bf16[8,272,1024]{2,1,0:T(8,128)(2,1)},...) custom-call(f32[8,272,1024]{2,1,0:T(8,128)} %get-tuple-element.130.m, ...), custom_call_target="tpu_custom_call", output_to_operand_aliasing={{13}: (17, {})} | custom-call | tf_op jit(solution)/shard_map/back/pallas_call | solution.py:977
  359.2 6.6 %copy.34 = bf16[8,257,1024]{2,0,1:T(8,128)(2,1)} copy(bf16[8,257,1024]{2,1,0:T(8,128)(2,1)} %get-tuple-element.177) | data formatting | bytes 8421376
  365.8 4.2 adds.7
  370.0 43.1 %wgrad.1 = (f32[2,2,2,4,128,512]{5,4,3,2,1,0:T(8,128)}, f32[2,2,128,512]{3,2,1,0:T(8,128)}, f32[2,2,128,512]{3,2,1,0:T(8,128)}, f32[2,2,128,512]{3,2,1,0:T(8,128...) custom-call(bf16[8,272,1024]{2,1,0:T(8,128)(2,1)} %get-tuple-element.148.refs_0_, ...), custom_call_target="tpu_custom_call", output_to_operand_aliasing={{5}: (8, {})} | custom-call | tf_op jit(solution)/shard_map/wgrad/pallas_call | solution.py:871
  413.1 99.8 %finish.1 = (bf16[257,8,1024]{2,1,0:T(8,128)(2,1)}, f32[128,3072]{1,0:T(8,128)}, f32[128,1024]{1,0:T(8,128)}, f32[128,4096]{1,0:T(8,128)}, f32[512,1024]{1,0:T(8,128)}, /*index=5*/f32[16,128]{1,0:T(8,128)}) custom-call(bf16[8,272,1024]{2,1,0:T(8,128)(2,1)} %get-tuple-element.93.x_ref, f32[8,272,1024]{2,1,0:T(8,128)} %get-tuple-element.144.gres_ref, ...), custom_call_target="tpu_custom_call" | custom-call | tf_op jit(solution)/shard_map/finish/pallas_call | solution.py:1186
  513.0 1.3 slice_bitcast_fusion
  514.2 1.3 slice_bitcast_fusion.1
  515.5 1.3 slice.27
  516.8 0.0 copy-start.2
  516.8 0.0 copy-start.3
  516.8 0.0 copy-start.1
  516.8 4.8 copy.56
  521.6 0.0 copy-done.2
  521.6 0.0 copy-start
  521.6 1.1 copy.57
  522.7 0.0 copy-done.3
  522.7 0.8 copy.58
  523.5 0.0 copy-done.1
  523.5 1.3 copy.59
  524.9 0.0 copy-done
  524.9 1.3 copy.60
Async XLA Ops:
  516.8 4.8 copy-start.2
  516.8 6.0 %copy-start.3 = (f32[128,1024]{1,0:T(8,128)S(1)}, f32[128,1024]{1,0:T(8,128)}, u32[]{:S(2)}) copy-start(f32[128,1024]{1,0:T(8,128)} %get-tuple-element.203) | copy-start | bytes 1572868
  516.8 6.8 %copy-start.1 = (f32[128,4096]{1,0:T(8,128)S(1)}, f32[128,4096]{1,0:T(8,128)}, u32[]{:S(2)}) copy-start(f32[128,4096]{1,0:T(8,128)} %get-tuple-element.204) | copy-start | bytes 6291460
  521.6 3.3 copy-start
where the time goes:
time: 535 us; the launch traced here: 527 us
  Pallas kernels  503 us (94%)
  local copies, waits for them, and re-layouts  21.4 us (4%)
    pallas_call x4, Pallas kernels, run_mlp(): pl.pallas_call(functools.partial(mlp_kernel, not acc, traffic), grid=(nbl...  176 us
    pallas_call x1, Pallas kernels, run_finish(): pl.pallas_call(finish_kernel, grid=(NSEQ,), in_specs=[tok] * 5 + [*map(wb...  99.8 us
    pallas_call x1, Pallas kernels, run_back(): pl.pallas_call(functools.partial(back_kernel, traffic), grid=(NSEQ,), in_...  64.9 us
    pallas_call x1, Pallas kernels, run_wgrad(): pl.pallas_call(functools.partial(wgrad_kernel, traffic), grid=(len(ORDER)...  43.1 us
    pallas_call x1, Pallas kernels, run_attn_fwd(): pl.pallas_call(functools.partial(attn_fwd_kernel, traffic), grid=(NSEQ,),...  38.8 us
    pallas_call x1, Pallas kernels, run_intake(): pl.pallas_call(intake_kernel, in_specs=[ANY] * 6 + [pl.BlockSpec(memory_s...  37.6 us
    pallas_call x1, Pallas kernels, run_qkv(): pl.pallas_call(functools.partial(qkv_kernel, traffic), grid=(NSEQ // bs,)...  23.8 us
    pallas_call x4, Pallas kernels, run_adds(): pl.pallas_call(functools.partial(adds_kernel, len(jobs)), grid=(4,), in_s...  19 us

commit v1 on v0

--- a/solution.py
+++ b/solution.py
@@ -714,7 +714,7 @@
                         lambda i: (0, 0, 0, jnp.clip(i - before, 0, n - 1), 0, 0))
 
 
-def mlp_kernel(first, traffic, h2_any, dm_any, wff_any, b1_ref, *refs):
+def mlp_kernel(first, row, traffic, h2_any, dm_any, wff_any, vec_ref, *refs):
     n_in, n_out, _ = traffic.sizes()
     if not first:
         m_in, dh_in, *refs = refs
@@ -760,7 +760,7 @@
         cw = 2 * LANES
         for c in range(QTR // cw):
             cols = slice(c * cw, (c + 1) * cw)
-            u = dot_nn(hb, w1[:, cols]) + b1_ref[:, cols]
+            u = dot_nn(hb, w1[:, cols]) + vec_ref[row:row + 1, cols]
             da = dot_nt(dmb, w2[cols])
             cdf = 0.5 + 0.5 * lax.erf(u * (0.5 ** 0.5))
             slope = cdf + u * (jnp.exp(-0.5 * u * u) * 0.3989422804014327)
@@ -783,16 +783,16 @@
     traffic.finish(i == pl.num_programs(0) - 1)
 
 
-def run_mlp(h2, dm, wff, b1, acc, cid, items=()):
+def run_mlp(h2, dm, vec, wff, quarter, acc, cid, items):
     traffic = Traffic(items, ("core",))
     bs = 2
     nblk = NSEQ // bs
     tok = pl.BlockSpec((bs, PAD, D), lambda i: (jnp.minimum(i, nblk - 1), 0, 0))
-    args = (h2, dm, wff, b1) + acc
+    args = (h2, dm, wff, vec) + acc
     base = len(args)
     outs = pl.pallas_call(
-        functools.partial(mlp_kernel, not acc, traffic), grid=(nblk + 4,),
-        in_specs=[ANY] * 3 + [fixed(b1.shape)] + [tok] * len(acc) + traffic.in_specs(),
+        functools.partial(mlp_kernel, not acc, V_UP + quarter, traffic), grid=(nblk + 4,),
+        in_specs=[ANY] * 3 + [fixed(vec.shape)] + [tok] * len(acc) + traffic.in_specs(),
         out_specs=[tok, tok, piece_spec(D, 2, nblk + 2), resident((8, QTR))] + traffic.out_specs(),
         out_shape=[act(dtype=F32), act(dtype=F32), f32s(2, 2, 2, 2, ROWS, HD), f32s(8, QTR)] + traffic.out_shapes(),
         scratch_shapes=[pltpu.VMEM(h2.shape, BF16), pltpu.VMEM(dm.shape, BF16), pltpu.VMEM((2, PEERS, ROWS, D), BF16),
@@ -806,7 +806,7 @@
 
 
 ORDER = ("part0", "part1", "mine0", "part2", "mine1", "part3", "mine2", "mine3")
-EARLY = 2
+EARLY = 3
 LOADED = ("o", "da", "h1", "dv", "dk", "dq")
 LOADED_AT = ("o da", "h1 dv", "", "dk", "", "dq")
 
@@ -1023,13 +1023,13 @@
 
 
 UNITS = DEPTH
-EVENTS = ("", "", "b0", "b1", "p00", "p01", "a2 p10 q00", "p11 q01")
-
-
-def finish_kernel(x_ref, gres_ref, dq_ref, dk_ref, dv_ref, wq_ref, wk_ref, wv_ref, vec_ref, ab_any, keep_ref, e0, e1,
-                  f0, f1, f2, p3_ref, b3_ref, sum_ref, hsum_ref, db0, db1, db2, db3,
+EVENTS = ("", "", "b0", "b1", "p00", "b2 p01", "p10 q00", "a3 p11 q01")
+
+
+def finish_kernel(x_ref, gres_ref, dq_ref, dk_ref, dv_ref, wall_any, f0, f1, f2, vec_ref, ab_any, keep_ref, e0, e1, e2,
+                  p3_ref, b3_ref, sum_ref, hsum_ref, db0, db1, db2, db3,
                   dx_ref, gqkv_ref, gout_ref, gup_ref, gdown_ref, small_ref,
-                  dx_s, ln_s, sk, r2, ra, rb, f3_s, small_s, all_p, part_s, all_z, ssem, rsem):
+                  w_s, f_s, load_sem, dx_s, ln_s, sk, r2, ra, rb, f3_s, small_s, all_p, part_s, all_z, ssem, rsem):
     i = pl.program_id(0)
     z, me = lax.axis_index("rep"), lax.axis_index("fsdp")
     sems, used = (ssem, rsem), []
@@ -1043,6 +1043,8 @@
           for u in range(EARLY, UNITS)}
     s2 = [[move(sk.at[u, color, 1], r2.at[u, color], partner(nm)) for color, nm in enumerate(NAMES["s2"])]
           for u in range(UNITS)]
+    w_loads = [pltpu.make_async_copy(wall_any.at[:, block(k)], w_s.at[k], load_sem.at[k]) for k in range(3)]
+    f_loads = [pltpu.make_async_copy(f, f_s.at[k], load_sem.at[3 + k]) for k, f in enumerate((f0, f1, f2))]
     near, far = partner("near"), partner("far")
     z_a = [[move(sk.at[u, c, 0], ra.at[u, c], near, *ROLES["zA"]) for c in colors] for u in range(UNITS)]
     z_b = [[move(ra.at[u, c], rb.at[u, c], far, *ROLES["zB"]) for c in colors] for u in range(UNITS)]
@@ -1104,10 +1106,14 @@
         def _():
             f3_s[:] = p3_ref[:] + b3_ref[:]
         start([f3_c])
-        for u, came in enumerate((e0, e1)):
+        for u, came in enumerate((e0, e1, e2)):
             after_s1(u, came)
         for u in s1:
             start(s1[u])
+        for cp in w_loads + f_loads:
+            cp.start()
+        for cp in w_loads:
+            cp.wait()
 
     act_on = {"a": after_s1, "b": after_s2, "p": after_za, "q": after_zb}
 
@@ -1121,8 +1127,8 @@
             handle(events)
 
     dh = None
-    for d_ref, w_ref in ((dq_ref, wq_ref), (dk_ref, wk_ref), (dv_ref, wv_ref)):
-        part = dot_nt(d_ref[:], w_ref[:].reshape(D, D))
+    for k, d_ref in enumerate((dq_ref, dk_ref, dv_ref)):
+        part = dot_nt(d_ref[:], w_s[k].reshape(D, D))
         dh = part if dh is None else dh + part
     g1, *_ = table_rows(vec_ref)
     xhat, rstd = ln_fwd(x_ref[:].astype(F32))
@@ -1142,24 +1148,24 @@
             small_s[to] = jnp.concatenate(mine, axis=0)
         start(plane_moves)
         all_p[me] = small_s[me]
-        handle("a3")
         for k in range(PEERS):
             dx_ref[:, :, block(k)] = dx_s[k].reshape(SEQ, NSEQ, LANES).astype(BF16)
-        handle("q10")
+        handle("q10 b3")
         arrive(plane_moves)
         part_s[:] = jnp.sum(all_p[:], axis=0)
         all_z[z] = part_s[:]
         start(column_moves)
-        handle("b2 q11")
-        for j, f_ref in enumerate((f0, f1, f2)):
-            store_ff(gup_ref, gdown_ref, f_ref, j)
-        handle("b3 p20")
+        handle("p20 q11")
+        for j, cp in enumerate(f_loads):
+            cp.wait()
+            store_ff(gup_ref, gdown_ref, f_s.at[j], j)
+        handle("p21 q20")
         arrive([f3_c])
         store_ff(gup_ref, gdown_ref, f3_s, 3)
         arrive(column_moves)
         small_ref[:] = jnp.sum(all_z[:], axis=0)
-        handle("p21 q20 p30")
-        handle("q21 p31 q30 q31")
+        handle("p30 q21")
+        handle("p31 q30 q31")
         for u, (out_ref, base) in enumerate(((gout_ref, 0), (gqkv_ref, 2 * D), (gqkv_ref, D), (gqkv_ref, 0))):
             for c in colors:
                 arrive(z_c[u][c:c + 1])
@@ -1175,17 +1181,18 @@
     def piece(*lead):
         return pltpu.VMEM(lead + (ROWS, HD), F32)
 
-    scratch = [pltpu.VMEM((PEERS, SEQ * NSEQ, LANES), F32), pltpu.VMEM((2, 8, D), F32)]
+    scratch = [pltpu.VMEM((3, PEERS, ROWS, D), BF16), piece(3, 2, 2), pltpu.SemaphoreType.DMA((6,))]
+    scratch += [pltpu.VMEM((PEERS, SEQ * NSEQ, LANES), F32), pltpu.VMEM((2, 8, D), F32)]
     scratch += [piece(UNITS, 2, 2)] + [piece(UNITS, 2)] * 3 + [piece(2, 2)]
     scratch += [pltpu.VMEM((PEERS, 16, LANES), F32)] * 2
     scratch += [pltpu.VMEM((16, LANES), F32), pltpu.VMEM((DEPTH, 16, LANES), F32)]
     scratch += [pltpu.SemaphoreType.DMA((64,)), pltpu.SemaphoreType.DMA((64,))]
     consts = [sums, hsum] + list(dbs)
-    held = [*early, *ffs, *last]
-    before = [xp, gres, *grads, wall, wall, wall, vec, ab, ab, *held]
+    held = [*early, *last]
+    before = [xp, gres, *grads, wall, *ffs, vec, ab, ab, *held]
     return pl.pallas_call(
         finish_kernel, grid=(NSEQ,),
-        in_specs=[tok] * 5 + [*map(wblk, range(3)), fixed(vec.shape), ANY, kept_spec(ab.shape)]
+        in_specs=[tok] * 5 + [ANY] * 4 + [fixed(vec.shape), ANY, kept_spec(ab.shape)]
         + [fixed(t.shape) for t in held + consts],
         out_specs=[fixed(sh) for sh in outs],
         out_shape=[jax.ShapeDtypeStruct(outs[0], BF16)] + [f32s(*sh) for sh in outs[1:]],
@@ -1198,28 +1205,27 @@
     vecs = jnp.concatenate([vec_params, b_up.reshape(-1, LANES), b_qkv.reshape(-1, LANES), jnp.zeros((1, LANES), F32)])
     xp, gp, wall, wo, c0, c1, c2, c3, vec = run_intake(
         x_loc.swapaxes(0, 1), dz_loc.swapaxes(0, 1), w_qkv, w_out, w_up, w_down, vecs, next(cid))
-    b1 = [vec[V_UP + j:V_UP + j + 1] for j in range(DEPTH)]
     own, rest = range(2)
     (h1, q, k, v), (wo,) = run_qkv(xp, wall, vec, next(cid), [Gather(wo, own, 2, 3)])
     (o, a, y, h2, dm, lse), (c0, c1) = run_attn_fwd(
         q, k, v, xp, gp, wo, vec, next(cid), [Gather(c0, own, 3, 5), Gather(c1, own, start=3)])
 
-    mlp = functools.partial(run_mlp, h2, dm)
-    acc, f0, db0, (c1, c2, c3) = mlp(c0, b1[0], (), next(cid), [Gather(c1, rest, 3), Gather(c2, own), Gather(c3, own)])
+    mlp = functools.partial(run_mlp, h2, dm, vec)
+    acc, f0, db0, (c1, c2, c3) = mlp(c0, 0, (), next(cid), [Gather(c1, rest, 3), Gather(c2, own), Gather(c3, own)])
     acc, f1, db1, (c2, c3, r0) = mlp(
-        c1, b1[1], acc, next(cid), [Gather(c2, rest, 3), Gather(c3, rest, 4), Chain(f0, "s1")])
+        c1, 1, acc, next(cid), [Gather(c2, rest, 3), Gather(c3, rest, 4), Chain(f0, "s1")])
     f0, = run_adds((f0, r0))
-    acc, f2, db2, (r0, r1) = mlp(c2, b1[2], acc, next(cid), [Chain(f0, "s2", ("zA", 2)), Chain(f1, "s1")])
+    acc, f2, db2, (r0, r1) = mlp(c2, 2, acc, next(cid), [Chain(f0, "s2", ("zA", 2)), Chain(f1, "s1")])
     f1, f0 = run_adds((f1, r1), r0)
     acc, f3, db3, (r1, r2, r0) = mlp(
-        c3, b1[3], acc, next(cid), [Chain(f1, "s2", ("zA", 2)), Chain(f2, "s1"), Chain(f0, "zB")])
+        c3, 3, acc, next(cid), [Chain(f1, "s2", ("zA", 2)), Chain(f2, "s1"), Chain(f0, "zB")])
     f2, f1, f0 = run_adds((f2, r2), r1, (f0, r0))
     m, dh = acc
     (z, gres, da, dq, dk, dv, sums, hsum), (r2, r3, f1, f0) = run_back(
         m, y, dh, a, gp, q, k, v, lse, wo, vec, next(cid),
-        [Chain(f2, "s2", ("zA", 2), ("zB", 4, 5)), Chain(f3, "s1", ("s2", 5)), Chain(f1, "zB", ("zC", 2, 4)), Chain(f0, "zC")])
+        [Chain(f2, "s2", ("zA", 2), ("zB", 4, 6)), Chain(f3, "s1", ("s2", 6)), Chain(f1, "zB", ("zC", 2, 4)), Chain(f0, "zC")])
     f3, f2 = run_adds(r3, r2)
-    ab, early, (r3, f2) = run_wgrad([o, da, h1, dv, dk, dq], next(cid), [Chain(f3, "zA", ("zB", 4, 7)), Chain(f2, "zC")])
+    ab, early, (r3, f2) = run_wgrad([o, da, h1, dv, dk, dq], next(cid), [Chain(f3, "zA", ("zB", 5, 7)), Chain(f2, "zC")])
     dx, g_qkv, g_out, g_up, g_down, small = run_finish(
         xp, gres, [dq, dk, dv], wall, vec, ab, early, [f0, f1, f2], r3, sums, hsum, [db0, db1, db2, db3], next(cid))
     g_bup, g_bqkv = small[V_UP:V_QKV].reshape(-1), small[V_QKV:V_QKV + 3].reshape(-1)

time: 535 us -> 530 us (level)
    pallas_call x5, Pallas kernels: 275 us -> 262 us  [the longest x4 175 us: run_mlp(): pl.pallas_call(functools.partial(mlp_kernel, not acc, V_UP + quarter, tra...]
    pallas_call x1, Pallas kernels: 43.1 us -> 54.6 us  [run_wgrad(): pl.pallas_call(functools.partial(wgrad_kernel, traffic), grid=(len(ORDER)...]
where the time goes in v1:
time: 530 us; the launch traced here: 522 us
  Pallas kernels  499 us (94%)
  local copies, waits for them, and re-layouts  19.9 us (4%)
    pallas_call x4, Pallas kernels, run_mlp(): pl.pallas_call(functools.partial(mlp_kernel, not acc, V_UP + quarter, tra...  175 us
    pallas_call x1, Pallas kernels, run_finish(): pl.pallas_call(finish_kernel, grid=(NSEQ,), in_specs=[tok] * 5 + [ANY] *...  87 us
    pallas_call x1, Pallas kernels, run_back(): pl.pallas_call(functools.partial(back_kernel, traffic), grid=(NSEQ,), in_...  63 us
    pallas_call x1, Pallas kernels, run_wgrad(): pl.pallas_call(functools.partial(wgrad_kernel, traffic), grid=(len(ORDER)...  54.6 us
    pallas_call x1, Pallas kernels, run_attn_fwd(): pl.pallas_call(functools.partial(attn_fwd_kernel, traffic), grid=(NSEQ,),...  38.8 us
    pallas_call x1, Pallas kernels, run_intake(): pl.pallas_call(intake_kernel, in_specs=[ANY] * 6 + [pl.BlockSpec(memory_s...  37.6 us
    pallas_call x1, Pallas kernels, run_qkv(): pl.pallas_call(functools.partial(qkv_kernel, traffic), grid=(NSEQ // bs,)...  23.8 us
    pallas_call x4, Pallas kernels, run_adds(): pl.pallas_call(functools.partial(adds_kernel, len(jobs)), grid=(4,), in_s...  19 us

profile of v1, /device:TPU:0, one launch (start us, length us, event | category | flops | bytes accessed | tf_op | source)
XLA Modules:
  0.0 521.6 jit_solution(3154725849333712462)
XLA Ops:
  0.6 0.1 pad.3.clone
  0.7 1.4 maximum_maximum_fusion.vecs
  2.1 37.6 %intake.1 = (bf16[8,272,1024]{2,1,0:T(8,128)(2,1)}, bf16[8,272,1024]{2,1,0:T(8,128)(2,1)}, bf16[8,384,1024]{2,1,0:T(8,128)(2,1)}, bf16[8,128,1024]{2,1,0:T(8,128...) custom-call(bf16[257,8,1024]{2,1,0:T(8,128)(2,1)} %bitcast.10, ...), custom_call_target="tpu_custom_call" | custom-call | tf_op jit(solution)/shard_map/intake/pallas_call | solution.py:505
  39.7 23.8 %qkv.1 = (bf16[8,272,1024]{2,1,0:T(8,128)(2,1)}, bf16[8,272,1024]{2,1,0:T(8,128)(2,1)}, bf16[8,272,1024]{2,1,0:T(8,128)(2,1)}, bf16[8,272,1024]{2,1,0:T(8,128)(2,1)}, bf16[8,128,1024]{2,1,0:T(8,128)(2,1)}) custom-call(bf16[8,272,1024]{2,1,0:T(8,128)(2,1)} %get-tuple-element.94.x_ref, ...), custom_call_target="tpu_custom_call", output_to_operand_aliasing={{4}: (5, {})} | custom-call | tf_op jit(solution)/shard_map/qkv/pallas_call | solution.py:540
  63.5 38.8 %attn_fwd.1 = (bf16[8,272,1024]{2,1,0:T(8,128)(2,1)}, f32[8,272,1024]{2,1,0:T(8,128)}, f32[8,272,1024]{2,1,0:T(8,128)}, bf16[8,272,1024]{2,1,0:T(8,128)(2,1)}, b...) custom-call(bf16[8,272,1024]{2,1,0:T(8,128)(2,1)} %get-tuple-element, ...), custom_call_target="tpu_custom_call", output_to_operand_aliasing={{6}: (7, {}), {7}: (8, {})} | custom-call | tf_op jit(solution)/shard_map/attn_fwd/pallas_call | solution.py:631
  102.4 42.3 %mlp.4 = (f32[8,272,1024]{2,1,0:T(8,128)}, f32[8,272,1024]{2,1,0:T(8,128)}, f32[2,2,2,2,128,512]{5,4,3,2,1,0:T(8,128)}, f32[8,1024]{1,0:T(8,128)}, bf16[8,256,10...) custom-call(bf16[8,272,1024]{2,1,0:T(8,128)(2,1)} %get-tuple-element, ...), custom_call_target="tpu_custom_call", output_to_operand_aliasing={{4}: (4, {}), {5}: (5, {}), {6}: (6, {})} | custom-call | tf_op jit(solution)/shard_map/mlp/pallas_call | solution.py:793
  144.6 43.6 %mlp.5 = (f32[8,272,1024]{2,1,0:T(8,128)}, f32[8,272,1024]{2,1,0:T(8,128)}, f32[2,2,2,2,128,512]{5,4,3,2,1,0:T(8,128)}, f32[8,1024]{1,0:T(8,128)}, bf16[8,256,10...) custom-call(bf16[8,272,1024]{2,1,0:T(8,128)(2,1)} %get-tuple-element, ...), custom_call_target="tpu_custom_call", output_to_operand_aliasing={{0}: (4, {}), {1}: (5, {}), {4}: (6, {}), {5}: (7, {})} | custom-call | tf_op jit(solution)/shard_map/mlp/pallas_call | solution.py:793
  188.2 4.2 adds.4.refs_2_.refs_3_
  192.4 45.3 %mlp.6 = (f32[8,272,1024]{2,1,0:T(8,128)}, f32[8,272,1024]{2,1,0:T(8,128)}, f32[2,2,2,2,128,512]{5,4,3,2,1,0:T(8,128)}, f32[8,1024]{1,0:T(8,128)}, f32[2,2,128,5...) custom-call(bf16[8,272,1024]{2,1,0:T(8,128)(2,1)} %get-tuple-element, ...), custom_call_target="tpu_custom_call", output_to_operand_aliasing={{0}: (4, {}), {1}: (5, {})} | custom-call | tf_op jit(solution)/shard_map/mlp/pallas_call | solution.py:793
  237.7 4.9 adds.5
  242.6 44.3 %mlp.7 = (f32[8,272,1024]{2,1,0:T(8,128)}, f32[8,272,1024]{2,1,0:T(8,128)}, f32[2,2,2,2,128,512]{5,4,3,2,1,0:T(8,128)}, f32[8,1024]{1,0:T(8,128)}, f32[2,2,128,5...) custom-call(bf16[8,272,1024]{2,1,0:T(8,128)(2,1)} %get-tuple-element, ...), custom_call_target="tpu_custom_call", output_to_operand_aliasing={{0}: (4, {}), {1}: (5, {})} | custom-call | tf_op jit(solution)/shard_map/mlp/pallas_call | solution.py:793
  286.9 5.7 %adds.6 = (f32[2,2,2,128,512]{4,3,2,1,0:T(8,128)}, f32[2,2,128,512]{3,2,1,0:T(8,128)}, f32[2,2,128,512]{3,2,1,0:T(8,128)}) custom-call(f32[2,2,2,2,128,512]{5,4,3,2,1,0:T(8,128)} %get-tuple-element.129.refs_4_.refs_0_, f32[2,2,2,128,512]{4,3,2,1,0:T(8,128)} %get-tuple-element.136.refs_1_, f32[2,2,128,512]{3,2,1,0:T(8,128)} %get-tuple-element.137.refs_2_, ...), custom_call_target="tpu_custom_call" | custom-call | tf_op jit(solution)/shard_map/adds/pallas_call | solution.py:1010
  292.6 63.0 %back.1 = (bf16[8,257,1024]{2,1,0:T(8,128)(2,1)}, f32[8,272,1024]{2,1,0:T(8,128)}, bf16[8,272,1024]{2,1,0:T(8,128)(2,1)}, bf16[8,272,1024]{2,1,0:T(8,128)(2,1)},...) custom-call(f32[8,272,1024]{2,1,0:T(8,128)} %get-tuple-element.131.m, ...), custom_call_target="tpu_custom_call", output_to_operand_aliasing={{13}: (17, {})} | custom-call | tf_op jit(solution)/shard_map/back/pallas_call | solution.py:977
  355.7 6.6 %copy.34 = bf16[8,257,1024]{2,0,1:T(8,128)(2,1)} copy(bf16[8,257,1024]{2,1,0:T(8,128)(2,1)} %get-tuple-element.179) | data formatting | bytes 8421376
  362.2 4.2 adds.7
  366.4 54.6 %wgrad.1 = (f32[2,2,2,4,128,512]{5,4,3,2,1,0:T(8,128)}, f32[2,2,128,512]{3,2,1,0:T(8,128)}, f32[2,2,128,512]{3,2,1,0:T(8,128)}, f32[2,2,128,512]{3,2,1,0:T(8,128...) custom-call(bf16[8,272,1024]{2,1,0:T(8,128)(2,1)} %get-tuple-element, ...), custom_call_target="tpu_custom_call", output_to_operand_aliasing={{6}: (8, {})} | custom-call | tf_op jit(solution)/shard_map/wgrad/pallas_call | solution.py:871
  421.0 87.0 %finish.1 = (bf16[257,8,1024]{2,1,0:T(8,128)(2,1)}, f32[128,3072]{1,0:T(8,128)}, f32[128,1024]{1,0:T(8,128)}, f32[128,4096]{1,0:T(8,128)}, f32[512,1024]{1,0:T(8,128)}, /*index=5*/f32[16,128]{1,0:T(8,128)}) custom-call(bf16[8,272,1024]{2,1,0:T(8,128)(2,1)} %get-tuple-element.94.x_ref, f32[8,272,1024]{2,1,0:T(8,128)} %get-tuple-element.145.gres_ref, ...), custom_call_target="tpu_custom_call" | custom-call | tf_op jit(solution)/shard_map/finish/pallas_call | solution.py:1193
  508.0 1.3 slice_bitcast_fusion
  509.2 1.3 slice_bitcast_fusion.1
  510.5 1.3 slice.11
  511.8 0.0 copy-start.2
  511.8 0.0 copy-start.3
  511.8 0.0 copy-start.1
  511.8 4.8 copy.56
  516.6 0.0 copy-done.2
  516.6 0.0 copy-start
  516.6 1.1 copy.57
  517.8 0.0 copy-done.3
  517.8 0.8 copy.58
  518.5 0.0 copy-done.1
  518.5 1.3 copy.59
  519.9 0.0 copy-done
  519.9 1.3 copy.60
Async XLA Ops:
  511.8 4.8 copy-start.2
  511.8 6.0 %copy-start.3 = (f32[128,1024]{1,0:T(8,128)S(1)}, f32[128,1024]{1,0:T(8,128)}, u32[]{:S(2)}) copy-start(f32[128,1024]{1,0:T(8,128)} %get-tuple-element.201) | copy-start | bytes 1572868
  511.8 6.8 %copy-start.1 = (f32[128,4096]{1,0:T(8,128)S(1)}, f32[128,4096]{1,0:T(8,128)}, u32[]{:S(2)}) copy-start(f32[128,4096]{1,0:T(8,128)} %get-tuple-element.202) | copy-start | bytes 6291460
  516.6 3.3 copy-start
